TPU v7x, 32 devices: a whole 2x2x4 slice. The times are simulated.
32 devices in a mesh: gx: 8 (over y, x, core), gy: 4 (over z).
Axes of the slice: x: 2, y: 2, z: 4, core: 2. Of those that a mesh axis runs over, the one named last changes fastest.
Arguments:
- layer_early: bfloat16 [1024, 8192], P(None, ('gx', 'gy')), may hold values from -48 to 48
- layer_late: bfloat16 [1024, 8192], P(('gx', 'gy')), may hold values from -48 to 48
Outputs:
- similarity: float32 [], replicated
- token_share: float32 [1024], P(('gx', 'gy'))
- early_rows: bfloat16 [1024, 8192], P(('gx', 'gy'))
- late_rows: bfloat16 [1024, 8192], P(('gx', 'gy'))
All inputs are finite; a program needn't handle non-finite values.
Results may differ from a plain program's by a relative error of at most 0.0015.
Values may be sent and summed in bfloat16 or wider, within the bound.
A program may use at most 128 MiB of HBM per device.

v0:
```python
import jax
import jax.numpy as jnp
from jax import lax
from jax.sharding import PartitionSpec as P


def pair_terms(left_early, left_late, right_early, right_late):
    dims = (((1,), (1,)), ((), ()))
    block_early = lax.dot_general(left_early, right_early, dims, preferred_element_type=jnp.float32)
    block_late = lax.dot_general(left_late, right_late, dims, preferred_element_type=jnp.float32)
    return (
        jnp.sum(block_early * block_late, axis=1),
        jnp.sum(block_early * block_early),
        jnp.sum(block_late * block_late),
    )


def body(layer_early, layer_late):
    total_rows = layer_early.shape[0]
    early_values = layer_early.astype(jnp.float32)
    early_cols = (early_values - jnp.mean(early_values, axis=0)).astype(jnp.bfloat16)
    late_values = layer_late.astype(jnp.float32)
    column_sums = lax.psum(jnp.sum(late_values, axis=0), ("gx", "gy"))
    late_rows = (late_values - column_sums / total_rows).astype(jnp.bfloat16)
    early_rows = lax.all_to_all(early_cols, ("gx", "gy"), split_axis=0, concat_axis=1, tiled=True)
    block_early, block_late = (
        lax.all_gather(early_rows, "gy", axis=0, tiled=True),
        lax.all_gather(late_rows, "gy", axis=0, tiled=True),
    )
    row_part, early_part, late_part = pair_terms(
        block_early,
        block_late,
        lax.all_gather(early_rows, "gx", axis=0, tiled=True),
        lax.all_gather(late_rows, "gx", axis=0, tiled=True),
    )
    own_align = lax.psum_scatter(row_part, "gy", scatter_dimension=0, tiled=True)
    total_kl, total_kk, total_ll = lax.psum(
        (jnp.sum(row_part), early_part, late_part), ("gx", "gy")
    )
    scale_norm = jnp.sqrt(total_kk * total_ll)
    similarity = total_kl / scale_norm
    token_share = total_rows * own_align / scale_norm
    return (similarity, token_share, early_rows, late_rows)


def solution(mesh):
    in_specs = (P(None, ("gx", "gy")), P(("gx", "gy"), None))
    out_specs = (P(), P(("gx", "gy")), P(("gx", "gy"), None), P(("gx", "gy"), None))
    return jax.shard_map(body, mesh=mesh, in_specs=in_specs, out_specs=out_specs, check_vma=False)
```

profile of v0, /device:TPU:0, one launch (start us, length us, event | category | flops | bytes accessed | tf_op | source)
XLA Modules:
  0.0 298.2 jit_solution(8457581897998979989)
XLA Ops:
  7.2 0.0 copy-start
  7.2 0.0 all-gather.9.cloned.1.call-start
  7.2 1.2 convert_reduce_fusion
  8.4 42.1 %psum.28 = f32[8192]{0:T(1024)S(1)} all-reduce(f32[8192]{0:T(1024)S(1)} %convert_reduce_fusion), channel_id=1, replica_groups=mesh['gx'=8,'gy'=4] {'gx','gy'}, use_global_device_ids=true, to_apply=%region_2.0 | all-reduce | flops 8192 | bytes 65536 | tf_op jit(solution)/shard_map/psum | solution.py:23
  50.6 1.9 fusion.1
  52.5 0.0 all-gather.9.cloned.1.call-update
  52.5 0.0 all-gather.11.cloned.1.call-start
  52.5 0.7 all-gather.11.cloned.1.call-update
  53.3 0.0 all-gather.5.cloned.1.call-start
  53.3 1.2 convert_reduce_fusion.1
  54.5 1.1 fusion
  55.6 28.2 %all_to_all.19 = bf16[32,32,256]{2,1,0:T(8,128)(2,1)S(1)} all-to-all(bf16[32,32,256]{2,1,0:T(8,128)(2,1)S(1)} %bitcast.12), channel_id=1, replica_groups=mesh['gx'=8,'gy'=4] {'gx','gy'}, dimensions={0} | all-to-all | bytes 1048576 | tf_op jit(solution)/shard_map/all_to_all | solution.py:25
  83.9 0.8 copy.8
  84.7 0.0 all-gather.5.cloned.1.call-update
  84.7 0.0 all-gather.7.cloned.1.call-start
  84.8 0.5 all-gather.7.cloned.1.call-update
  85.3 0.0 copy-done
  85.3 0.6 dynamic-slice
  86.6 22.4 %all-gather.9.cloned.1.call-done = bf16[128,8192]{1,0:T(8,128)(2,1)} async-done(((bf16[32,8192]{1,0:T(8,128)(2,1)}), bf16[128,8192]{1,0:T(8,128)(2,1)}) %all-gather.9.cloned.1.call-update) | async-done | bytes 2097168 | tf_op jit(solution)/shard_map/all_gather | solution.py:28
  109.0 38.1 %all-gather.11.cloned.1.call-done = bf16[256,8192]{1,0:T(8,128)(2,1)} async-done(((bf16[32,8192]{1,0:T(8,128)(2,1)}), bf16[256,8192]{1,0:T(8,128)(2,1)}) %all-gather.11.cloned.1.call-update) | async-done | bytes 4194320 | tf_op jit(solution)/shard_map/all_gather | solution.py:34
  147.1 4.4 %fusion.3 = f32[128,256]{1,0:T(8,128)S(1)} fusion(bf16[128,8192]{1,0:T(8,128)(2,1)} %all-gather.9.cloned.1.call-done, bf16[256,8192]{1,0:T(8,128)(2,1)} %all-gather.11.cloned.1.call-done), kind=kOutput, calls=%fused_computation.14 | convolution fusion | flops 536870912 | bytes 6422528 | tf_op jit(solution)/shard_map/dot_general | solution.py:10
  151.5 43.5 %all-gather.5.cloned.1.call-done = bf16[128,8192]{1,0:T(8,128)(2,1)} async-done(((bf16[32,8192]{1,0:T(8,128)(2,1)}), bf16[128,8192]{1,0:T(8,128)(2,1)}) %all-gather.5.cloned.1.call-update) | async-done | bytes 2097168 | tf_op jit(solution)/shard_map/all_gather | solution.py:27
  195.0 37.7 %all-gather.7.cloned.1.call-done = bf16[256,8192]{1,0:T(8,128)(2,1)} async-done(((bf16[32,8192]{1,0:T(8,128)(2,1)}), bf16[256,8192]{1,0:T(8,128)(2,1)}) %all-gather.7.cloned.1.call-update) | async-done | bytes 4194320 | tf_op jit(solution)/shard_map/all_gather | solution.py:33
  232.7 5.0 %multiply_reduce_fusion.2 = (f32[128]{0:T(128)S(1)}, f32[]{:T(128)}, f32[]{:T(128)}, f32[]{:T(128)}) fusion(f32[128,256]{1,0:T(8,128)S(1)} %fusion.3, bf16[128,8192]{1,0:T(8,128)(2,1)} %all-gather.5.cloned.1.call-done, bf16[256,8192]{1,0:T(8,128)(2,1)} %all-gather.7.cloned.1.call-done), kind=kOutput, calls=%fused_computation.8 | convolution fusion | flops 537100160 | bytes 6423052 | tf_op jit(solution)/shard_map/dot_general | solution.py:9
  237.7 39.6 %all-reduce.1 = (f32[]{:T(128)}, f32[]{:T(128)}, f32[]{:T(128)}) all-reduce(f32[]{:T(128)} %get-tuple-element.5, f32[]{:T(128)} %get-tuple-element.7, f32[]{:T(128)} %get-tuple-element.6), channel_id=1, replica_groups=mesh['gx'=8,'gy'=4] {'gx','gy'}, use_global_device_ids=true, to_apply=%region_4.0 | all-reduce | flops 3 | bytes 24 | tf_op jit(solution)/shard_map/psum | solution.py:37
  278.7 10.6 %all-reduce = f32[128]{0:T(128)S(1)} all-reduce(f32[128]{0:T(128)S(1)} %get-tuple-element.4), channel_id=2, replica_groups=mesh['gx'=8,'gy'=4] {'gy'}, use_global_device_ids=true, to_apply=%region_10.0.clone | all-reduce | flops 128 | bytes 1024
  290.0 0.6 fusion.2
  (2 shorter events, 0.0 us)
Async XLA Ops:
  7.2 78.2 %copy-start = (u32[32]{0:T(128)S(1)}, u32[32]{0:T(128)}, u32[]{:S(2)}) copy-start(u32[32]{0:T(128)} %constant.11) | copy-start | bytes 388
  7.2 101.8 %all-gather.9.cloned.1.call-start = ((), (), s32[]{:S(2)}) async-start(), calls=%async_computation.3 | async-start | bytes 2621440 | tf_op jit(solution)/shard_map/all_gather | solution.py:28
  52.5 94.6 %all-gather.11.cloned.1.call-start = ((), (), s32[]{:S(2)}) async-start(), calls=%async_computation.4 | async-start | bytes 4718592 | tf_op jit(solution)/shard_map/all_gather | solution.py:34
  53.3 141.7 %all-gather.5.cloned.1.call-start = ((), (), s32[]{:S(2)}) async-start(), calls=%async_computation.1 | async-start | bytes 2621440 | tf_op jit(solution)/shard_map/all_gather | solution.py:27
  84.7 147.9 %all-gather.7.cloned.1.call-start = ((), (), s32[]{:S(2)}) async-start(), calls=%async_computation.2 | async-start | bytes 4718592 | tf_op jit(solution)/shard_map/all_gather | solution.py:33
Sparse Core Ops, SparseCore 0:
  52.6 56.3 all-gather.8
  111.5 35.5 all-gather.10
  149.3 45.6 all-gather.4
  197.3 35.3 all-gather.6
where the time goes:
time: 299 us; the launch traced here: 298 us
  waiting for transfers between devices  143 us (48%)
  blocking collectives  121 us (40%)
  between operations  17.6 us (6%)
  matrix products  9.4 us (3%)
  other arithmetic  6.03 us (2%)
    all_gather x1, waiting for transfers between devices, body(): lax.all_gather(early_rows, 'gy', axis=0, tiled=True)  43.5 us
    psum x1, blocking collectives, body(): column_sums = lax.psum(jnp.sum(late_values, axis=0), ('gx', 'gy'))  42.1 us
    psum x1, blocking collectives, body(): lax.psum((jnp.sum(row_part), early_part, late_part), ('gx', 'gy'))  39.6 us
    all_gather x1, waiting for transfers between devices, body(): lax.all_gather(late_rows, 'gx', axis=0, tiled=True)  38.1 us
    all_gather x1, waiting for transfers between devices, body(): lax.all_gather(early_rows, 'gx', axis=0, tiled=True)  37.7 us
    all_to_all x1, blocking collectives, body(): lax.all_to_all(early_cols, ('gx', 'gy'), split_axis=0, concat_axis=1, til...  28.2 us
    all_gather x1, waiting for transfers between devices, body(): lax.all_gather(late_rows, 'gy', axis=0, tiled=True)  22.4 us
    unnamed x1, blocking collectives  10.6 us
  transfers between devices with their start and end apart: 4, of which 4 were waited for; matrix products, arithmetic and copies ran while one was open for 3% of the time, Pallas kernels for 0%

commit v1 on v0

--- a/solution.py
+++ b/solution.py
@@ -20,7 +20,7 @@
     early_values = layer_early.astype(jnp.float32)
     early_cols = (early_values - jnp.mean(early_values, axis=0)).astype(jnp.bfloat16)
     late_values = layer_late.astype(jnp.float32)
-    column_sums = lax.psum(jnp.sum(late_values, axis=0), ("gx", "gy"))
+    column_sums = lax.psum(lax.psum(jnp.sum(late_values, axis=0), "gy"), "gx")
     late_rows = (late_values - column_sums / total_rows).astype(jnp.bfloat16)
     early_rows = lax.all_to_all(early_cols, ("gx", "gy"), split_axis=0, concat_axis=1, tiled=True)
     block_early, block_late = (

time: 299 us -> 297 us (level)
    psum x1 -> x2, blocking collectives: 42.1 us -> 43.2 us  [body(): column_sums = lax.psum(lax.psum(jnp.sum(late_values, axis=0), 'gy'), 'gx')]
where the time goes in v1:
time: 297 us
  waiting for transfers between devices  143 us (48%)
  blocking collectives  119 us (40%)
  between operations  17.6 us (6%)
  matrix products  9.4 us (3%)
  other arithmetic  6.03 us (2%)
    all_gather x1, waiting for transfers between devices, body(): lax.all_gather(early_rows, 'gy', axis=0, tiled=True)  43.5 us
    psum x2, blocking collectives, body(): column_sums = lax.psum(lax.psum(jnp.sum(late_values, axis=0), 'gy'), 'gx')  43.2 us
    psum x1, blocking collectives, body(): lax.psum((jnp.sum(row_part), early_part, late_part), ('gx', 'gy'))  39.6 us
    all_gather x1, waiting for transfers between devices, body(): lax.all_gather(late_rows, 'gx', axis=0, tiled=True)  38.1 us
    all_gather x1, waiting for transfers between devices, body(): lax.all_gather(early_rows, 'gx', axis=0, tiled=True)  37.7 us
    all_to_all x1, blocking collectives, body(): lax.all_to_all(early_cols, ('gx', 'gy'), split_axis=0, concat_axis=1, til...  25.7 us
    all_gather x1, waiting for transfers between devices, body(): lax.all_gather(late_rows, 'gy', axis=0, tiled=True)  22.4 us
    unnamed x1, blocking collectives  10.6 us
  transfers between devices with their start and end apart: 4, of which 4 were waited for; matrix products, arithmetic and copies ran while one was open for 3% of the time, Pallas kernels for 0%

profile of v1, /device:TPU:0, one launch (start us, length us, event | category | flops | bytes accessed | tf_op | source)
XLA Modules:
  0.0 296.7 jit_solution(4108128390334790932)
XLA Ops:
  7.2 0.0 copy-start
  7.2 0.0 all-gather.9.cloned.1.call-start
  7.2 1.2 convert_reduce_fusion
  8.4 20.8 %psum.35 = f32[8192]{0:T(1024)S(1)} all-reduce(f32[8192]{0:T(1024)S(1)} %convert_reduce_fusion), channel_id=1, replica_groups=mesh['gx'=8,'gy'=4] {'gy'}, use_global_device_ids=true, to_apply=%region_2.0 | all-reduce | flops 8192 | bytes 65536 | tf_op jit(solution)/shard_map/psum | solution.py:23
  29.2 22.4 %psum.36 = f32[8192]{0:T(1024)S(1)} all-reduce(f32[8192]{0:T(1024)S(1)} %psum.35), channel_id=1, replica_groups=mesh['gx'=8,'gy'=4] {'gx'}, use_global_device_ids=true, to_apply=%region_3.0 | all-reduce | flops 8192 | bytes 65536 | tf_op jit(solution)/shard_map/psum | solution.py:23
  51.6 1.9 fusion.1
  53.5 0.0 all-gather.9.cloned.1.call-update
  53.5 0.0 all-gather.11.cloned.1.call-start
  53.6 0.7 all-gather.11.cloned.1.call-update
  54.3 0.0 all-gather.5.cloned.1.call-start
  54.3 1.2 convert_reduce_fusion.1
  55.5 1.1 fusion
  56.7 25.7 %all_to_all.19 = bf16[32,32,256]{2,1,0:T(8,128)(2,1)S(1)} all-to-all(bf16[32,32,256]{2,1,0:T(8,128)(2,1)S(1)} %bitcast.12), channel_id=1, replica_groups=mesh['gx'=8,'gy'=4] {'gx','gy'}, dimensions={0} | all-to-all | bytes 1048576 | tf_op jit(solution)/shard_map/all_to_all | solution.py:25
  82.4 0.8 copy.8
  83.2 0.0 all-gather.5.cloned.1.call-update
  83.3 0.0 all-gather.7.cloned.1.call-start
  83.3 0.5 all-gather.7.cloned.1.call-update
  83.9 0.0 copy-done
  83.9 0.6 dynamic-slice
  85.1 22.4 %all-gather.9.cloned.1.call-done = bf16[128,8192]{1,0:T(8,128)(2,1)} async-done(((bf16[32,8192]{1,0:T(8,128)(2,1)}), bf16[128,8192]{1,0:T(8,128)(2,1)}) %all-gather.9.cloned.1.call-update) | async-done | bytes 2097168 | tf_op jit(solution)/shard_map/all_gather | solution.py:28
  107.5 38.1 %all-gather.11.cloned.1.call-done = bf16[256,8192]{1,0:T(8,128)(2,1)} async-done(((bf16[32,8192]{1,0:T(8,128)(2,1)}), bf16[256,8192]{1,0:T(8,128)(2,1)}) %all-gather.11.cloned.1.call-update) | async-done | bytes 4194320 | tf_op jit(solution)/shard_map/all_gather | solution.py:34
  145.6 4.4 %fusion.3 = f32[128,256]{1,0:T(8,128)S(1)} fusion(bf16[128,8192]{1,0:T(8,128)(2,1)} %all-gather.9.cloned.1.call-done, bf16[256,8192]{1,0:T(8,128)(2,1)} %all-gather.11.cloned.1.call-done), kind=kOutput, calls=%fused_computation.14 | convolution fusion | flops 536870912 | bytes 6422528 | tf_op jit(solution)/shard_map/dot_general | solution.py:10
  150.0 43.5 %all-gather.5.cloned.1.call-done = bf16[128,8192]{1,0:T(8,128)(2,1)} async-done(((bf16[32,8192]{1,0:T(8,128)(2,1)}), bf16[128,8192]{1,0:T(8,128)(2,1)}) %all-gather.5.cloned.1.call-update) | async-done | bytes 2097168 | tf_op jit(solution)/shard_map/all_gather | solution.py:27
  193.5 37.7 %all-gather.7.cloned.1.call-done = bf16[256,8192]{1,0:T(8,128)(2,1)} async-done(((bf16[32,8192]{1,0:T(8,128)(2,1)}), bf16[256,8192]{1,0:T(8,128)(2,1)}) %all-gather.7.cloned.1.call-update) | async-done | bytes 4194320 | tf_op jit(solution)/shard_map/all_gather | solution.py:33
  231.2 5.0 %multiply_reduce_fusion.2 = (f32[128]{0:T(128)S(1)}, f32[]{:T(128)}, f32[]{:T(128)}, f32[]{:T(128)}) fusion(f32[128,256]{1,0:T(8,128)S(1)} %fusion.3, bf16[128,8192]{1,0:T(8,128)(2,1)} %all-gather.5.cloned.1.call-done, bf16[256,8192]{1,0:T(8,128)(2,1)} %all-gather.7.cloned.1.call-done), kind=kOutput, calls=%fused_computation.8 | convolution fusion | flops 537100160 | bytes 6423052 | tf_op jit(solution)/shard_map/dot_general | solution.py:9
  236.3 39.6 %all-reduce.1 = (f32[]{:T(128)}, f32[]{:T(128)}, f32[]{:T(128)}) all-reduce(f32[]{:T(128)} %get-tuple-element.5, f32[]{:T(128)} %get-tuple-element.7, f32[]{:T(128)} %get-tuple-element.6), channel_id=1, replica_groups=mesh['gx'=8,'gy'=4] {'gx','gy'}, use_global_device_ids=true, to_apply=%region_5.0 | all-reduce | flops 3 | bytes 24 | tf_op jit(solution)/shard_map/psum | solution.py:37
  277.2 10.6 %all-reduce = f32[128]{0:T(128)S(1)} all-reduce(f32[128]{0:T(128)S(1)} %get-tuple-element.4), channel_id=2, replica_groups=mesh['gx'=8,'gy'=4] {'gy'}, use_global_device_ids=true, to_apply=%region_11.0.clone | all-reduce | flops 128 | bytes 1024
  288.5 0.6 fusion.2
  (2 shorter events, 0.0 us)
Async XLA Ops:
  7.2 76.7 %copy-start = (u32[32]{0:T(128)S(1)}, u32[32]{0:T(128)}, u32[]{:S(2)}) copy-start(u32[32]{0:T(128)} %constant.11) | copy-start | bytes 388
  7.2 100.4 %all-gather.9.cloned.1.call-start = ((), (), s32[]{:S(2)}) async-start(), calls=%async_computation.3 | async-start | bytes 2621440 | tf_op jit(solution)/shard_map/all_gather | solution.py:28
  53.5 92.1 %all-gather.11.cloned.1.call-start = ((), (), s32[]{:S(2)}) async-start(), calls=%async_computation.4 | async-start | bytes 4718592 | tf_op jit(solution)/shard_map/all_gather | solution.py:34
  54.3 139.2 %all-gather.5.cloned.1.call-start = ((), (), s32[]{:S(2)}) async-start(), calls=%async_computation.1 | async-start | bytes 2621440 | tf_op jit(solution)/shard_map/all_gather | solution.py:27
  83.3 147.9 %all-gather.7.cloned.1.call-start = ((), (), s32[]{:S(2)}) async-start(), calls=%async_computation.2 | async-start | bytes 4718592 | tf_op jit(solution)/shard_map/all_gather | solution.py:33
Sparse Core Ops, SparseCore 0:
  53.6 53.8 all-gather.8
  110.0 35.5 all-gather.10
  147.8 45.6 all-gather.4
  195.8 35.3 all-gather.6

commit v2 on v0

--- a/solution.py
+++ b/solution.py
@@ -31,7 +31,9 @@
         block_early,
         block_late,
         lax.all_gather(early_rows, "gx", axis=0, tiled=True),
-        lax.all_gather(late_rows, "gx", axis=0, tiled=True),
+        jnp.concatenate(
+            lax.all_to_all(jnp.stack([late_rows] * lax.axis_size("gx")), "gx", 0, 0), axis=0
+        ),
     )
     own_align = lax.psum_scatter(row_part, "gy", scatter_dimension=0, tiled=True)
     total_kl, total_kk, total_ll = lax.psum(

time: 299 us -> 259 us (0.87)
  waiting for transfers between devices: 143 us -> 95.1 us
  starting transfers between devices: 0.16 us -> 6.65 us
    all_gather x1 -> x0, waiting for transfers between devices: 38.1 us -> none  [body(): lax.all_gather(late_rows, 'gx', axis=0, tiled=True)]
    all_gather x1, waiting for transfers between devices: 43.5 us -> 7.98 us  [body(): lax.all_gather(early_rows, 'gy', axis=0, tiled=True)]
    all_to_all x0 -> x1, waiting for transfers between devices: none -> 34.4 us  [body(): lax.all_to_all(jnp.stack([late_rows] * lax.axis_size('gx')), 'gx', 0, 0)]
    all_gather x1, waiting for transfers between devices: 22.4 us -> 14 us  [body(): lax.all_gather(late_rows, 'gy', axis=0, tiled=True)]
    all_to_all x0 -> x1, starting transfers between devices: none -> 6.53 us  [body(): lax.all_to_all(jnp.stack([late_rows] * lax.axis_size('gx')), 'gx', 0, 0)]
  transfers between devices with their start and end apart: 4 -> 4, of which waited for: 4 -> 4; matrix products, arithmetic and copies ran while one was open for 3% -> 4% of each run, Pallas kernels for 0% -> 0%
where the time goes in v2:
time: 259 us
  blocking collectives  120 us (46%)
  waiting for transfers between devices  95.1 us (37%)
  between operations  17.6 us (7%)
  matrix products  9.42 us (4%)
  starting transfers between devices  6.65 us (3%)
  other arithmetic  6.07 us (2%)
  local copies, waits for them, and re-layouts  3.87 us (1%)
    psum x1, blocking collectives, body(): column_sums = lax.psum(jnp.sum(late_values, axis=0), ('gx', 'gy'))  42.1 us
    psum x1, blocking collectives, body(): lax.psum((jnp.sum(row_part), early_part, late_part), ('gx', 'gy'))  39.6 us
    all_gather x1, waiting for transfers between devices, body(): lax.all_gather(early_rows, 'gx', axis=0, tiled=True)  37.9 us
    all_to_all x1, waiting for transfers between devices, body(): lax.all_to_all(jnp.stack([late_rows] * lax.axis_size('gx')), 'gx', 0, 0)  34.4 us
    all_to_all x1, blocking collectives, body(): lax.all_to_all(early_cols, ('gx', 'gy'), split_axis=0, concat_axis=1, til...  27.6 us
    all_gather x1, waiting for transfers between devices, body(): lax.all_gather(late_rows, 'gy', axis=0, tiled=True)  14 us
    unnamed x1, blocking collectives  10.6 us
    all_gather x1, waiting for transfers between devices, body(): lax.all_gather(early_rows, 'gy', axis=0, tiled=True)  7.98 us
  transfers between devices with their start and end apart: 4, of which 4 were waited for; matrix products, arithmetic and copies ran while one was open for 4% of the time, Pallas kernels for 0%

profile of v2, /device:TPU:0, one launch (start us, length us, event | category | flops | bytes accessed | tf_op | source)
XLA Modules:
  0.0 258.6 jit_solution(11675752291317669171)
XLA Ops:
  7.2 0.0 all-gather.8.cloned.1.call-start
  7.2 1.2 convert_reduce_fusion
  8.4 42.1 %psum.28 = f32[8192]{0:T(1024)S(1)} all-reduce(f32[8192]{0:T(1024)S(1)} %convert_reduce_fusion), channel_id=1, replica_groups=mesh['gx'=8,'gy'=4] {'gx','gy'}, use_global_device_ids=true, to_apply=%region_2.0 | all-reduce | flops 8192 | bytes 65536 | tf_op jit(solution)/shard_map/psum | solution.py:23
  50.5 1.9 fusion.1
  52.5 0.0 copy-start
  52.5 0.0 all-gather.8.cloned.1.call-update
  52.5 0.0 all-gather.4.cloned.1.call-start
  52.5 1.2 convert_reduce_fusion.1
  53.8 1.1 fusion
  54.9 27.6 %all_to_all.24 = bf16[32,32,256]{2,1,0:T(8,128)(2,1)S(1)} all-to-all(bf16[32,32,256]{2,1,0:T(8,128)(2,1)S(1)} %bitcast.13), channel_id=1, replica_groups=mesh['gx'=8,'gy'=4] {'gx','gy'}, dimensions={0} | all-to-all | bytes 1048576 | tf_op jit(solution)/shard_map/all_to_all | solution.py:25
  82.5 0.8 copy.8
  83.3 0.0 all-gather.4.cloned.1.call-update
  83.3 0.0 all-gather.6.cloned.1.call-start
  83.4 0.7 all-gather.6.cloned.1.call-update
  84.1 0.0 copy-done
  84.1 2.5 stack.2
  86.5 0.0 copy-start.1
  86.5 6.5 %all-to-all-start.1 = ((bf16[8,32,8192]{2,1,0:T(8,128)(2,1)}), bf16[8,32,8192]{2,1,0:T(8,128)(2,1)}, u32[]{:S(2)}, u32[]{:S(2)}) async-start(bf16[8,32,8192]{2,1,0:T(8,128)(2,1)} %stack.2), calls=%async_computation.1 | async-start | bytes 8388608 | tf_op jit(solution)/shard_map/all_to_all | solution.py:35
  93.1 0.0 copy-done.1
  93.1 0.6 dynamic-slice
  94.3 14.0 %all-gather.8.cloned.1.call-done = bf16[128,8192]{1,0:T(8,128)(2,1)} async-done(((bf16[32,8192]{1,0:T(8,128)(2,1)}), bf16[128,8192]{1,0:T(8,128)(2,1)}) %all-gather.8.cloned.1.call-update) | async-done | bytes 2097168 | tf_op jit(solution)/shard_map/all_gather | solution.py:28
  108.3 34.4 %all-to-all-done.1 = bf16[8,32,8192]{2,1,0:T(8,128)(2,1)} async-done(((bf16[8,32,8192]{2,1,0:T(8,128)(2,1)}), bf16[8,32,8192]{2,1,0:T(8,128)(2,1)}, u32[]{:S(2)}, u32[]{:S(2)}) %all-to-all-start.1) | async-done | bytes 4194336 | tf_op jit(solution)/shard_map/all_to_all | solution.py:35
  142.8 4.4 %fusion.3 = f32[128,256]{1,0:T(8,128)S(1)} fusion(bf16[128,8192]{1,0:T(8,128)(2,1)} %all-gather.8.cloned.1.call-done, bf16[256,8192]{1,0:T(8,128)(2,1)} %bitcast.2), kind=kOutput, calls=%fused_computation.14 | convolution fusion | flops 536870912 | bytes 6422528 | tf_op jit(solution)/shard_map/dot_general | solution.py:10
  147.2 8.0 %all-gather.4.cloned.1.call-done = bf16[128,8192]{1,0:T(8,128)(2,1)} async-done(((bf16[32,8192]{1,0:T(8,128)(2,1)}), bf16[128,8192]{1,0:T(8,128)(2,1)}) %all-gather.4.cloned.1.call-update) | async-done | bytes 2097168 | tf_op jit(solution)/shard_map/all_gather | solution.py:27
  155.1 37.9 %all-gather.6.cloned.1.call-done = bf16[256,8192]{1,0:T(8,128)(2,1)} async-done(((bf16[32,8192]{1,0:T(8,128)(2,1)}), bf16[256,8192]{1,0:T(8,128)(2,1)}) %all-gather.6.cloned.1.call-update) | async-done | bytes 4194320 | tf_op jit(solution)/shard_map/all_gather | solution.py:33
  193.0 5.0 %multiply_reduce_fusion.2 = (f32[128]{0:T(128)S(1)}, f32[]{:T(128)}, f32[]{:T(128)}, f32[]{:T(128)}) fusion(f32[128,256]{1,0:T(8,128)S(1)} %fusion.3, bf16[128,8192]{1,0:T(8,128)(2,1)} %all-gather.4.cloned.1.call-done, bf16[256,8192]{1,0:T(8,128)(2,1)} %all-gather.6.cloned.1.call-done), kind=kOutput, calls=%fused_computation.8 | convolution fusion | flops 537100160 | bytes 6423052 | tf_op jit(solution)/shard_map/dot_general | solution.py:9
  198.1 39.6 %all-reduce.1 = (f32[]{:T(128)}, f32[]{:T(128)}, f32[]{:T(128)}) all-reduce(f32[]{:T(128)} %get-tuple-element.5, f32[]{:T(128)} %get-tuple-element.7, f32[]{:T(128)} %get-tuple-element.6), channel_id=1, replica_groups=mesh['gx'=8,'gy'=4] {'gx','gy'}, use_global_device_ids=true, to_apply=%region_4.0 | all-reduce | flops 3 | bytes 24 | tf_op jit(solution)/shard_map/psum | solution.py:39
  239.0 10.6 %all-reduce = f32[128]{0:T(128)S(1)} all-reduce(f32[128]{0:T(128)S(1)} %get-tuple-element.4), channel_id=2, replica_groups=mesh['gx'=8,'gy'=4] {'gy'}, use_global_device_ids=true, to_apply=%region_10.0.clone | all-reduce | flops 128 | bytes 1024
  250.3 0.6 fusion.2
  (2 shorter events, 0.0 us)
Async XLA Ops:
  7.2 101.2 %all-gather.8.cloned.1.call-start = ((), (), s32[]{:S(2)}) async-start(), calls=%async_computation.4 | async-start | bytes 2621440 | tf_op jit(solution)/shard_map/all_gather | solution.py:28
  52.5 31.6 %copy-start = (bf16[32,8192]{1,0:T(8,128)(2,1)S(1)}, bf16[32,8192]{1,0:T(8,128)(2,1)}, u32[]{:S(2)}) copy-start(bf16[32,8192]{1,0:T(8,128)(2,1)} %fusion.1) | copy-start | bytes 1572868
  52.5 102.7 %all-gather.4.cloned.1.call-start = ((), (), s32[]{:S(2)}) async-start(), calls=%async_computation.2 | async-start | bytes 2621440 | tf_op jit(solution)/shard_map/all_gather | solution.py:27
  83.3 109.7 %all-gather.6.cloned.1.call-start = ((), (), s32[]{:S(2)}) async-start(), calls=%async_computation.3 | async-start | bytes 4718592 | tf_op jit(solution)/shard_map/all_gather | solution.py:33
  86.5 6.5 %copy-start.1 = (u32[32]{0:T(128)S(1)}, u32[32]{0:T(128)}, u32[]{:S(2)}) copy-start(u32[32]{0:T(128)} %constant.11) | copy-start | bytes 388
  86.5 56.2 %all-to-all-start.1 = ((bf16[8,32,8192]{2,1,0:T(8,128)(2,1)}), bf16[8,32,8192]{2,1,0:T(8,128)(2,1)}, u32[]{:S(2)}, u32[]{:S(2)}) async-start(bf16[8,32,8192]{2,1,0:T(8,128)(2,1)} %stack.2), calls=%async_computation.1 | async-start | bytes 8388608 | tf_op jit(solution)/shard_map/all_to_all | solution.py:35
Sparse Core Ops, SparseCore 0:
  52.6 55.6 all-gather.7
  110.5 44.6 all-gather.3
  157.6 35.3 all-gather.5
